TPU v7x, 32 devices: a whole 2x2x4 slice. The times are simulated.
32 devices in a mesh: parts: 2 (over y), mem: 4 (over z), space: 4 (over x, core).
Axes of the slice: x: 2, y: 2, z: 4, core: 2. Of those that a mesh axis runs over, the one named last changes fastest.
Arguments:
- ensemble: bfloat16 [64, 70, 8192], P('mem', None, ('parts', 'space')), parts along dimension 2, may hold values from -6 to 6
- transform: bfloat16 [128, 64], P('parts'), parts along dimension 0, may hold values from -0.75 to 0.75
- obs_operator: bfloat16 [16, 70], replicated, may hold values from -0.75 to 0.75
- obs_weight: float32 [16, 8192], P(None, ('parts', 'space')), parts along dimension 1, may hold values from 0.25 to 40, as said below
Outputs:
- analysis: bfloat16 [64, 70, 8192], P('mem', None, ('parts', 'space')), parts along dimension 2
- prior_gram: float32 [128, 64], P('parts'), parts along dimension 0
- posterior_gram: float32 [128, 64], P('parts'), parts along dimension 0
There are 2 independent parts, one for each index of `parts`. A program takes and returns all parts, laid end to end along the dimension named above; an argument that names none is the same for every part. Nothing has to cross between parts.
Inputs may be any that keep to these rules, and one draw needn't show every extreme that they name: `obs_weight`: positive.
All inputs are finite; a program needn't handle non-finite values.
Results may differ from a plain program's by a relative error of at most 0.001.
Values may be sent and summed in bfloat16 or wider, within the bound.
A program may use at most 64 MiB of HBM per device.

v0:
```python
import jax
import jax.numpy as jnp
from jax import lax
from jax.sharding import PartitionSpec as P

MEMBERS = 64
HIGHEST = lax.Precision.HIGHEST


def gram_terms(observed, weights):
    departures = observed - jnp.sum(observed, axis=0) / MEMBERS
    weighted = departures * weights[None, :, :]
    partial_gram = jnp.einsum("ioc,joc->ij", weighted, departures, precision=HIGHEST)
    return (partial_gram, jnp.sum(weights))


def per_device(ensemble, transform, obs_operator, obs_weight):
    local_members = ensemble.shape[0]
    mixing = transform.astype(jnp.float32)
    own_start = lax.axis_index("mem") * local_members
    own_columns = lax.dynamic_slice_in_dim(transform, own_start, local_members, 1)
    keep_mean = 1.0 - jnp.sum(own_columns.astype(jnp.float32), axis=0)
    members_block = lax.all_gather(ensemble, "mem", axis=0, tiled=True)
    combined = jnp.einsum(
        "kj,kvc->jvc", own_columns, members_block, preferred_element_type=jnp.float32
    )
    totals = jnp.sum(members_block, axis=0, dtype=jnp.float32)
    results = (totals, combined)
    totals = results[0]
    combined = results[1]
    member_mean = totals / MEMBERS
    analysis = (combined + member_mean[None, :, :] * keep_mean[:, None, None]).astype(jnp.bfloat16)
    observed = jnp.einsum("ov,mvc->moc", obs_operator, ensemble, preferred_element_type=jnp.float32)
    by_columns = lax.all_to_all(
        observed.astype(jnp.bfloat16), "mem", split_axis=2, concat_axis=0, tiled=True
    ).astype(observed.dtype)
    cells_here = by_columns.shape[2]
    own_weights = lax.dynamic_slice_in_dim(
        obs_weight, lax.axis_index("mem") * cells_here, cells_here, 1
    )
    partial_gram, weight_sum = gram_terms(by_columns, own_weights)
    gram_sum, weight_total = lax.psum((partial_gram, weight_sum), ("mem", "space"))
    prior_gram = gram_sum / weight_total
    carried = jnp.dot(mixing.T, prior_gram, precision=HIGHEST)
    posterior_gram = jnp.dot(carried, mixing, precision=HIGHEST)
    return (analysis, prior_gram, posterior_gram)


def solution(mesh):
    return jax.shard_map(
        per_device,
        mesh=mesh,
        in_specs=(
            P("mem", None, ("parts", "space")),
            P("parts", None),
            P(),
            P(None, ("parts", "space")),
        ),
        out_specs=(P("mem", None, ("parts", "space")), P("parts", None), P("parts", None)),
        check_vma=False,
    )
```

profile of v0, /device:TPU:0, one launch (start us, length us, event | category | flops | bytes accessed | tf_op | source)
XLA Modules:
  0.0 202.9 jit_solution(353153275937876548)
XLA Ops:
  7.2 0.7 all-gather.2.cloned.1.call-update
  7.9 3.0 %fusion.7 = bf16[16,16,1024]{2,1,0:T(8,128)(2,1)S(1)} fusion(bf16[16,70,1024]{2,0,1:T(8,128)(2,1)} %param.4, bf16[16,70]{1,0:T(8,128)(2,1)} %param.6), kind=kOutput, calls=%fused_computation.8 | convolution fusion | flops 36962304 | bytes 2820288 | tf_op jit(solution)/shard_map/ov,mvc->moc/dot_general | solution.py:33
  10.9 4.7 %copy.25 = bf16[16,16,1024]{1,0,2:T(8,128)(2,1)} copy(bf16[16,16,1024]{2,1,0:T(8,128)(2,1)S(1)} %fusion.7) | data formatting | bytes 1048576 | tf_op jit(solution)/shard_map/convert_element_type | solution.py:35
  15.6 6.6 %reshape.27 = bf16[4,2,32768]{2,1,0:T(2,128)(2,1)} reshape(bf16[1024,16,16]{2,1,0:T(8,128)(2,1)} %bitcast.28) | data formatting | bytes 1048576
  22.2 6.4 %all-to-all-start = ((bf16[4,2,32768]{2,1,0:T(2,128)(2,1)}), bf16[4,2,32768]{2,1,0:T(2,128)(2,1)S(1)}, u32[]{:S(2)}, u32[]{:S(2)}) async-start(bf16[4,2,32768]{2,1,0:T(2,128)(2,1)} %reshape.27), calls=%async_computation | async-start | bytes 1048576 | tf_op jit(solution)/shard_map/all_to_all | solution.py:34
  28.6 0.1 constant_dynamic-slice_fusion.1
  28.7 0.1 copy.28
  28.8 0.1 convert_reduce_fusion.2
  28.9 1.3 fusion.16
  30.2 25.9 %all-to-all-done = bf16[4,2,32768]{2,1,0:T(2,128)(2,1)S(1)} async-done(((bf16[4,2,32768]{2,1,0:T(2,128)(2,1)}), bf16[4,2,32768]{2,1,0:T(2,128)(2,1)S(1)}, u32[]{:S(2)}, u32[]{:S(2)}) %all-to-all-start) | async-done | bytes 524320 | tf_op jit(solution)/shard_map/all_to_all | solution.py:34
  56.1 4.1 %reshape.28 = bf16[1024,16,16]{2,1,0:T(8,128)(2,1)} reshape(bf16[4,2,32768]{2,1,0:T(2,128)(2,1)S(1)} %all-to-all-done) | data formatting | bytes 1048576
  60.2 6.1 %bitcast_convert_fusion = f32[16,16,1024]{1,0,2:T(8,128)} fusion(bf16[1024,16,16]{2,1,0:T(8,128)(2,1)} %reshape.28), kind=kLoop, calls=%fused_computation.22 | loop fusion | flops 262144 | bytes 1572864 | tf_op jit(solution)/shard_map/convert_element_type | solution.py:36
  66.4 6.6 %copy.26 = f32[4,16,16,256]{3,1,0,2:T(8,128)S(1)} copy(f32[4,16,16,256]{2,1,3,0:T(8,128)} %bitcast.27) | data formatting | bytes 2097152 | tf_op jit(solution)/shard_map/convert_element_type | solution.py:36
  72.9 4.2 %convert_reduce_fusion.1 = f32[16,1024]{0,1:T(8,128)S(1)} fusion(bf16[1024,16,16]{2,1,0:T(8,128)(2,1)} %reshape.28), kind=kLoop, calls=%fused_computation.4 | loop fusion | flops 507904 | bytes 589824 | tf_op jit(solution)/shard_map/reduce_sum | solution.py:11
  77.2 0.1 copy.27
  77.3 0.1 bitcast_subtract_fusion
  77.5 1.0 fusion.10
  78.5 63.8 %all-reduce = (f32[64,64]{1,0:T(8,128)S(1)}, f32[]{:T(128)}) all-reduce(f32[64,64]{1,0:T(8,128)S(1)} %fusion.10, f32[]{:T(128)} %get-tuple-element.5), channel_id=1, replica_groups=mesh['parts'=2,'mem'=4,'space'=4] {'mem','space'}, use_global_device_ids=true, to_apply=%region_4.0 | all-reduce | flops 4097 | bytes 32776 | tf_op jit(solution)/shard_map/psum | solution.py:42
  142.3 0.7 broadcast_divide_fusion
  142.9 0.2 fusion.17
  143.2 0.8 fusion.18
  144.0 42.6 %all-gather.2.cloned.1.call-done = bf16[64,70,1024]{2,0,1:T(8,128)(2,1)} async-done(((bf16[16,70,1024]{2,0,1:T(8,128)(2,1)}), bf16[64,70,1024]{2,0,1:T(8,128)(2,1)}) %all-gather.2.cloned.1.call-update) | async-done | bytes 9175056 | tf_op jit(solution)/shard_map/all_gather | solution.py:23
  186.6 6.7 %convert_reduce_fusion = f32[70,1024]{1,0:T(8,128)S(1)} fusion(bf16[64,70,1024]{2,0,1:T(8,128)(2,1)} %all-gather.2.cloned.1.call-done), kind=kLoop, calls=%fused_computation | loop fusion | flops 9103360 | bytes 9461760 | tf_op jit(solution)/shard_map/reduce_sum | solution.py:27
  193.3 2.8 %add_convert_fusion = bf16[16,70,1024]{2,0,1:T(8,128)(2,1)} fusion(f32[16]{0:T(128)S(1)} %broadcast_subtract_fusion, f32[70,1024]{1,0:T(8,128)S(1)} %broadcast_multiply_fusion, bf16[64,70,1024]{2,0,1:T(8,128)(2,1)S(1)} %copy-done.1, bf16[64,16]{1,0:T(8,128)(2,1)S(1)} %constant_dynamic-slice_fusion.1), kind=kOutput, calls=%fused_computation.1 | convolution fusion | flops 150241280 | bytes 11757632 | tf_op jit(solution)/shard_map/kj,kvc->jvc/dot_general | solution.py:24
  (11 shorter events, 0.1 us)
Async XLA Ops:
  7.2 21.4 %copy-start = (bf16[64,64]{1,0:T(8,128)(2,1)S(1)}, bf16[64,64]{1,0:T(8,128)(2,1)}, u32[]{:S(2)}) copy-start(bf16[64,64]{1,0:T(8,128)(2,1)} %param.5) | copy-start | bytes 24580
  7.2 179.4 %all-gather.2.cloned.1.call-start = ((), (), s32[]{:S(2)}) async-start(), calls=%async_computation.1 | async-start | bytes 11468800 | tf_op jit(solution)/shard_map/all_gather | solution.py:23
  22.2 33.9 %all-to-all-start = ((bf16[4,2,32768]{2,1,0:T(2,128)(2,1)}), bf16[4,2,32768]{2,1,0:T(2,128)(2,1)S(1)}, u32[]{:S(2)}, u32[]{:S(2)}) async-start(bf16[4,2,32768]{2,1,0:T(2,128)(2,1)} %reshape.27), calls=%async_computation | async-start | bytes 1048576 | tf_op jit(solution)/shard_map/all_to_all | solution.py:34
  142.9 50.3 %copy-start.2 = (f32[64,64]{1,0:T(8,128)}, f32[64,64]{1,0:T(8,128)S(1)}, u32[]{:S(2)}) copy-start(f32[64,64]{1,0:T(8,128)S(1)} %broadcast_divide_fusion) | copy-start | bytes 49156
  186.6 6.7 %copy-start.1 = (bf16[64,70,1024]{2,0,1:T(8,128)(2,1)S(1)}, bf16[64,70,1024]{2,0,1:T(8,128)(2,1)}, u32[]{:S(2)}) copy-start(bf16[64,70,1024]{2,0,1:T(8,128)(2,1)} %all-gather.2.cloned.1.call-done) | copy-start | bytes 27525124
Sparse Core Ops, SparseCore 0:
  9.6 176.9 all-gather.1
where the time goes:
time: 203 us
  waiting for transfers between devices  69.2 us (34%)
  blocking collectives  63.8 us (31%)
  local copies, waits for them, and re-layouts  22.2 us (11%)
  other arithmetic  19.3 us (10%)
  between operations  14.1 us (7%)
  matrix products  7.83 us (4%)
  starting transfers between devices  6.41 us (3%)
    psum x1, blocking collectives, per_device(): lax.psum((partial_gram, weight_sum), ('mem', 'space'))  63.8 us
    all_gather x1, waiting for transfers between devices, per_device(): members_block = lax.all_gather(ensemble, 'mem', axis=0, tiled=True)  42.6 us
    all_to_all x1, waiting for transfers between devices, per_device(): lax.all_to_all(observed.astype(jnp.bfloat16), 'mem', split_axis=2, concat...  25.9 us
    unnamed x9, local copies, waits for them, and re-layouts  10.8 us
    reduce_sum x1, other arithmetic, per_device(): totals = jnp.sum(members_block, axis=0, dtype=jnp.float32)  6.65 us
    convert_element_type x1, local copies, waits for them, and re-layouts, per_device(): by_columns = lax.all_to_all(observed.astype(jnp.bfloat16), 'mem', split_a...  6.59 us
    all_to_all x1, starting transfers between devices, per_device(): lax.all_to_all(observed.astype(jnp.bfloat16), 'mem', split_axis=2, concat...  6.38 us
    convert_element_type x1, other arithmetic, per_device(): by_columns = lax.all_to_all(observed.astype(jnp.bfloat16), 'mem', split_a...  6.11 us
  transfers between devices with their start and end apart: 2, of which 2 were waited for; matrix products, arithmetic and copies ran while one was open for 20% of the time, Pallas kernels for 0%

commit v1 on v0

--- a/solution.py
+++ b/solution.py
@@ -31,9 +31,10 @@
     member_mean = totals / MEMBERS
     analysis = (combined + member_mean[None, :, :] * keep_mean[:, None, None]).astype(jnp.bfloat16)
     observed = jnp.einsum("ov,mvc->moc", obs_operator, ensemble, preferred_element_type=jnp.float32)
-    by_columns = lax.all_to_all(
-        observed.astype(jnp.bfloat16), "mem", split_axis=2, concat_axis=0, tiled=True
-    ).astype(observed.dtype)
+    update_matrix_all = lambda target: jnp.concatenate(
+        lax.all_to_all(jnp.stack(jnp.split(target, lax.axis_size("mem"), 2), 0), "mem", 0, 0), 0
+    )
+    by_columns = update_matrix_all(observed.astype(jnp.bfloat16)).astype(observed.dtype)
     cells_here = by_columns.shape[2]
     own_weights = lax.dynamic_slice_in_dim(
         obs_weight, lax.axis_index("mem") * cells_here, cells_here, 1

time: 203 us -> 198 us (0.975)
  local copies, waits for them, and re-layouts: 22.2 us -> 0.21 us
  waiting for transfers between devices: 69.2 us -> 89.9 us
  other arithmetic: 19.3 us -> 9.92 us
  blocking collectives: 63.8 us -> 68.2 us
    all_gather x1, waiting for transfers between devices: 42.6 us -> 66 us  [per_device(): members_block = lax.all_gather(ensemble, 'mem', axis=0, tiled=True)]
    convert_element_type x2 -> x0, local copies, waits for them, and re-layouts: 11.3 us -> none  [the longest x1 6.59 us: per_device(): by_columns = lax.all_to_all(observed.astype(jnp.bfloat16), 'mem', split_a...]
    unnamed x9 -> x7, local copies, waits for them, and re-layouts: 10.8 us -> 0.1 us
    convert_element_type x1, other arithmetic: 6.11 us -> 0.17 us  [per_device(): update_matrix_all(observed.astype(jnp.bfloat16)).astype(observed.dtype)]
    psum x1, blocking collectives: 63.8 us -> 68.2 us  [per_device(): lax.psum((partial_gram, weight_sum), ('mem', 'space'))]
    reduce_sum x2 -> x1, other arithmetic: 4.27 us -> 0.1 us  [gram_terms(): departures = observed - jnp.sum(observed, axis=0) / MEMBERS]
    all_to_all x1, waiting for transfers between devices: 25.9 us -> 23.1 us  [per_device(): lax.all_to_all(jnp.stack(jnp.split(target, lax.axis_size('mem'), 2), 0),...]
  transfers between devices with their start and end apart: 2 -> 2, of which waited for: 2 -> 2; matrix products, arithmetic and copies ran while one was open for 20% -> 5% of each run, Pallas kernels for 0% -> 0%
where the time goes in v1:
time: 198 us
  waiting for transfers between devices  89.9 us (45%)
  blocking collectives  68.2 us (34%)
  between operations  14.1 us (7%)
  other arithmetic  9.92 us (5%)
  matrix products  8.91 us (4%)
  starting transfers between devices  6.38 us (3%)
    psum x1, blocking collectives, per_device(): lax.psum((partial_gram, weight_sum), ('mem', 'space'))  68.2 us
    all_gather x1, waiting for transfers between devices, per_device(): members_block = lax.all_gather(ensemble, 'mem', axis=0, tiled=True)  66 us
    all_to_all x1, waiting for transfers between devices, per_device(): lax.all_to_all(jnp.stack(jnp.split(target, lax.axis_size('mem'), 2), 0),...  23.1 us
    reduce_sum x1, other arithmetic, per_device(): totals = jnp.sum(members_block, axis=0, dtype=jnp.float32)  6.65 us
    all_to_all x1, starting transfers between devices, per_device(): lax.all_to_all(jnp.stack(jnp.split(target, lax.axis_size('mem'), 2), 0),...  6.35 us
  transfers between devices with their start and end apart: 2, of which 2 were waited for; matrix products, arithmetic and copies ran while one was open for 5% of the time, Pallas kernels for 0%

profile of v1, /device:TPU:0, one launch (start us, length us, event | category | flops | bytes accessed | tf_op | source)
XLA Modules:
  0.0 197.6 jit_solution(8026389074448474218)
XLA Ops:
  7.2 0.0 copy-start
  7.2 0.0 all-gather.2.cloned.1.call-start
  7.2 0.7 all-gather.2.cloned.1.call-update
  7.9 3.0 %fusion.7 = bf16[16,16,1024]{2,1,0:T(8,128)(2,1)S(1)} fusion(bf16[16,70,1024]{2,0,1:T(8,128)(2,1)} %param.4, bf16[16,70]{1,0:T(8,128)(2,1)} %param.6), kind=kOutput, calls=%fused_computation.7 | convolution fusion | flops 36962304 | bytes 2820288 | tf_op jit(solution)/shard_map/ov,mvc->moc/dot_general | solution.py:33
  10.9 0.9 pad_maximum_fusion
  11.8 6.3 %all-to-all-start = ((bf16[4,16,16,256]{3,2,1,0:T(8,128)(2,1)}), bf16[4,16,16,256]{3,2,1,0:T(8,128)(2,1)S(1)}, u32[]{:S(2)}, u32[]{:S(2)}) async-start(bf16[4,16,16,256]{3,2,1,0:T(8,128)(2,1)} %pad_maximum_fusion), calls=%async_computation | async-start | bytes 1048576 | tf_op jit(solution)/shard_map/all_to_all | solution.py:35
  18.2 0.0 copy-done
  18.2 0.1 constant_dynamic-slice_fusion.1
  18.2 0.1 copy.10
  18.3 0.1 convert_reduce_fusion.2
  18.4 1.3 fusion.17
  19.8 23.1 %all-to-all-done = bf16[4,16,16,256]{3,2,1,0:T(8,128)(2,1)S(1)} async-done(((bf16[4,16,16,256]{3,2,1,0:T(8,128)(2,1)}), bf16[4,16,16,256]{3,2,1,0:T(8,128)(2,1)S(1)}, u32[]{:S(2)}, u32[]{:S(2)}) %all-to-all-start) | async-done | bytes 524320 | tf_op jit(solution)/shard_map/all_to_all | solution.py:35
  42.9 0.1 convert_reduce_fusion.1
  43.0 0.2 bitcast_convert_fusion
  43.2 2.1 %fusion.10 = f32[64,64]{1,0:T(8,128)S(1)} fusion(f32[64,16,256]{2,1,0:T(8,128)S(1)} %bitcast_convert_fusion, f32[16,256]{1,0:T(8,128)S(1)} %get-tuple-element.6, f32[16,256]{1,0:T(8,128)S(1)} %broadcast_multiply_fusion.1), kind=kOutput, calls=%fused_computation.8 | convolution fusion | flops 202113024 | bytes 1097728 | tf_op jit(solution)/shard_map/ioc,joc->ij/dot_general | solution.py:13
  45.3 68.2 %all-reduce = (f32[64,64]{1,0:T(8,128)S(1)}, f32[]{:T(128)}) all-reduce(f32[64,64]{1,0:T(8,128)S(1)} %fusion.10, f32[]{:T(128)} %get-tuple-element.5), channel_id=1, replica_groups=mesh['parts'=2,'mem'=4,'space'=4] {'mem','space'}, use_global_device_ids=true, to_apply=%region_3.0 | all-reduce | flops 4097 | bytes 32776 | tf_op jit(solution)/shard_map/psum | solution.py:43
  113.5 0.7 broadcast_divide_fusion
  114.2 0.0 copy-start.2
  114.2 0.2 fusion.18
  114.4 0.8 fusion.19
  115.3 66.0 %all-gather.2.cloned.1.call-done = bf16[64,70,1024]{2,0,1:T(8,128)(2,1)} async-done(((bf16[16,70,1024]{2,0,1:T(8,128)(2,1)}), bf16[64,70,1024]{2,0,1:T(8,128)(2,1)}) %all-gather.2.cloned.1.call-update) | async-done | bytes 9175056 | tf_op jit(solution)/shard_map/all_gather | solution.py:23
  181.3 6.7 %convert_reduce_fusion = f32[70,1024]{1,0:T(8,128)S(1)} fusion(bf16[64,70,1024]{2,0,1:T(8,128)(2,1)} %all-gather.2.cloned.1.call-done), kind=kLoop, calls=%fused_computation | loop fusion | flops 9103360 | bytes 9461760 | tf_op jit(solution)/shard_map/reduce_sum | solution.py:27
  187.9 0.0 copy-done.2
  188.0 2.8 %add_convert_fusion = bf16[16,70,1024]{2,0,1:T(8,128)(2,1)} fusion(f32[16]{0:T(128)S(1)} %broadcast_subtract_fusion, f32[70,1024]{1,0:T(8,128)S(1)} %broadcast_multiply_fusion, bf16[64,70,1024]{2,0,1:T(8,128)(2,1)S(1)} %copy-done.1, bf16[64,16]{1,0:T(8,128)(2,1)S(1)} %constant_dynamic-slice_fusion.1), kind=kOutput, calls=%fused_computation.1 | convolution fusion | flops 150241280 | bytes 11757632 | tf_op jit(solution)/shard_map/kj,kvc->jvc/dot_general | solution.py:24
  (6 shorter events, 0.1 us)
Async XLA Ops:
  7.2 11.0 %copy-start = (bf16[64,64]{1,0:T(8,128)(2,1)S(1)}, bf16[64,64]{1,0:T(8,128)(2,1)}, u32[]{:S(2)}) copy-start(bf16[64,64]{1,0:T(8,128)(2,1)} %param.5) | copy-start | bytes 24580
  7.2 174.1 %all-gather.2.cloned.1.call-start = ((), (), s32[]{:S(2)}) async-start(), calls=%async_computation.1 | async-start | bytes 11468800 | tf_op jit(solution)/shard_map/all_gather | solution.py:23
  11.8 31.1 %all-to-all-start = ((bf16[4,16,16,256]{3,2,1,0:T(8,128)(2,1)}), bf16[4,16,16,256]{3,2,1,0:T(8,128)(2,1)S(1)}, u32[]{:S(2)}, u32[]{:S(2)}) async-start(bf16[4,16,16,256]{3,2,1,0:T(8,128)(2,1)} %pad_maximum_fusion), calls=%async_computation | async-start | bytes 1048576 | tf_op jit(solution)/shard_map/all_to_all | solution.py:35
  114.2 73.8 %copy-start.2 = (f32[64,64]{1,0:T(8,128)}, f32[64,64]{1,0:T(8,128)S(1)}, u32[]{:S(2)}) copy-start(f32[64,64]{1,0:T(8,128)S(1)} %broadcast_divide_fusion) | copy-start | bytes 49156
  181.3 6.7 %copy-start.1 = (bf16[64,70,1024]{2,0,1:T(8,128)(2,1)S(1)}, bf16[64,70,1024]{2,0,1:T(8,128)(2,1)}, u32[]{:S(2)}) copy-start(bf16[64,70,1024]{2,0,1:T(8,128)(2,1)} %all-gather.2.cloned.1.call-done) | copy-start | bytes 27525124
Sparse Core Ops, SparseCore 0:
  9.6 171.6 all-gather.1
